TPU v7x, 32 devices: a whole 2x2x4 slice. The times are simulated.
32 devices in a mesh: groups: 2 (over x), seq: 16 (over z, y, core).
Axes of the slice: x: 2, y: 2, z: 4, core: 2. Of those that a mesh axis runs over, the one named last changes fastest.
Arguments:
- queries: bfloat16 [64, 128, 576], P('groups', 'seq'), parts along dimension 0, may hold values from -8 to 8
- prefix_pool: bfloat16 [1024, 64, 576], P(('groups', 'seq')), parts along dimension 0, may hold values from -6 to 6
- block_table: int32 [8, 128], P('groups'), parts along dimension 0, may hold values from 0 to 511, as said below
- prefix_of: int32 [64], P('groups'), parts along dimension 0, may hold values from 0 to 3
- suffix_cache: bfloat16 [64, 2048, 576], P('groups', 'seq'), parts along dimension 0, may hold values from -24 to 24
- suffix_len: int32 [64], P('groups'), parts along dimension 0, may hold values from 2 to 2048
Outputs:
- context: bfloat16 [64, 128, 512], P('groups', 'seq'), parts along dimension 0
There are 2 independent parts, one for each index of `groups`. A program takes and returns all parts, laid end to end along the dimension named above; each array names one. Nothing has to cross between parts.
Inputs may be any that keep to these rules, and one draw needn't show every extreme that they name: `block_table`: each of the 512 pool blocks is named exactly once in the table, and of each aligned run of 32 pool blocks exactly 8 belong to each prefix.
All inputs are finite; a program needn't handle non-finite values.
Results may differ from a plain program's by a relative error of at most 0.0033.
Values may be sent and summed in bfloat16 or wider, within the bound.
A program may use at most 128 MiB of HBM per device.

v0:
```python
import jax
import jax.numpy as jnp
from jax import lax
from jax.sharding import PartitionSpec as P

LAT = 512


score_scale = 192.0 ** (-0.5)


def body(queries, prefix_pool, block_table, prefix_of, suffix_cache, suffix_len):
    blocks_here, block_rows, channels = prefix_pool.shape
    prefix_total = block_table.shape[0]
    slots_here = suffix_cache.shape[1]
    position = lax.axis_index("seq")
    block_ids = position * blocks_here + lax.iota(jnp.int32, blocks_here)
    owners = jnp.any(block_table[:, :, None] == block_ids[None, None, :], axis=1)
    prefix_ids = lax.iota(jnp.int32, prefix_total)
    labels = jnp.sum(owners.astype(jnp.int32) * prefix_ids[:, None], axis=0)
    order = jnp.argsort(labels, stable=True)
    segment_rows = blocks_here // prefix_total * block_rows
    segments = prefix_pool[order].reshape(prefix_total, segment_rows, channels)
    request_keys = jnp.concatenate([segments[prefix_of], suffix_cache], axis=1)
    slot_ids = position * slots_here + lax.iota(jnp.int32, slots_here)
    live_slots = slot_ids[None, :] < suffix_len[:, None]
    visible = jnp.concatenate(
        [jnp.ones((live_slots.shape[0], segment_rows), bool), live_slots], axis=1
    )
    scores = (
        jnp.einsum(
            "rhw,rkw->rhk",
            lax.all_gather(queries, "seq", axis=1, tiled=True),
            request_keys,
            preferred_element_type=jnp.float32,
        )
        * score_scale
    )
    scores = jnp.where(visible[:, None, :], scores, -jnp.inf)
    highest = lax.pmax(jnp.max(scores, axis=2), "seq")
    weights = jnp.exp(scores - highest[:, :, None])
    weight_sum = jnp.sum(weights, axis=2)
    rounded = weights.astype(jnp.bfloat16)
    weighted = jnp.einsum(
        "rhk,rkl->rhl", rounded, request_keys[:, :, :LAT], preferred_element_type=jnp.float32
    )
    weight_sum, weighted = (
        lax.psum_scatter(weight_sum, "seq", scatter_dimension=1, tiled=True),
        lax.psum_scatter(weighted, "seq", scatter_dimension=1, tiled=True),
    )
    return (weighted / weight_sum[:, :, None]).astype(jnp.bfloat16)


def solution(mesh):
    return jax.shard_map(
        body,
        mesh=mesh,
        in_specs=(
            P("groups", "seq", None),
            P(("groups", "seq"), None, None),
            P("groups", None),
            P("groups"),
            P("groups", "seq", None),
            P("groups"),
        ),
        out_specs=P("groups", "seq", None),
        check_vma=False,
    )
```

profile of v0, /device:TPU:0, one launch (start us, length us, event | category | flops | bytes accessed | tf_op | source)
XLA Modules:
  0.0 271.6 jit_solution(3408118859675830077)
XLA Ops:
  6.5 0.0 copy-start
  6.5 0.0 all-gather.2.cloned.1.call-start
  6.5 0.7 all-gather.2.cloned.1.call-update
  7.3 0.0 reduce-scatter.3.cloned.1.call-start
  7.3 0.9 compare_reduce_fusion
  8.2 1.6 sort.17
  9.9 0.7 compare_select_fusion
  10.5 0.0 copy-done
  10.5 2.4 gather_fusion
  12.9 2.9 %copy.17 = bf16[4,512,576]{1,2,0:T(8,128)(2,1)S(1)} copy(bf16[4,512,576]{2,1,0:T(8,128)(2,1)} %bitcast.16) | data formatting | bytes 4718592 | tf_op jit(solution)/shard_map/reshape | solution.py:23
  15.8 0.0 copy-start.2
  15.9 7.8 %gather_fusion.1 = bf16[32,512,576]{1,2,0:T(8,128)(2,1)} fusion(bf16[4,512,576]{1,2,0:T(8,128)(2,1)S(1)} %copy.17, s32[1024]{0:T(1024)S(1)} %get-tuple-element.9), kind=kCustom, calls=%fused_computation.1 | custom fusion | bytes 37748864 | tf_op jit(solution)/shard_map/gather | solution.py:24
  23.7 0.0 copy-done.2
  23.7 0.1 broadcast_compare_fusion
  23.8 16.9 %constant_dynamic-update-slice_fusion.1 = bf16[32,640,576]{1,2,0:T(8,128)(2,1)} fusion(bf16[32,512,576]{1,2,0:T(8,128)(2,1)} %gather_fusion.1), kind=kLoop, calls=%fused_computation.20 | loop fusion | bytes 37748736
  40.7 5.0 %constant_dynamic-update-slice_fusion = bf16[32,640,576]{1,2,0:T(8,128)(2,1)} fusion(bf16[32,640,576]{1,2,0:T(8,128)(2,1)} %constant_dynamic-update-slice_fusion.1, bf16[32,128,576]{1,2,0:T(8,128)(2,1)} %param.10), kind=kLoop, calls=%fused_computation.19 | loop fusion | bytes 9437184 | tf_op jit(solution)/shard_map/concatenate | solution.py:24
  45.7 22.9 %all-gather.2.cloned.1.call-done = bf16[32,128,576]{2,1,0:T(8,128)(2,1)} async-done(((bf16[32,8,576]{2,1,0:T(8,128)(2,1)}), bf16[32,128,576]{2,1,0:T(8,128)(2,1)}) %all-gather.2.cloned.1.call-update) | async-done | bytes 4718608 | tf_op jit(solution)/shard_map/all_gather | solution.py:33
  68.5 17.1 %bitcast_reduce_fusion = (f32[32,128]{1,0:T(8,128)S(1)}, f32[32,640,128]{2,1,0:T(8,128)}) fusion(pred[32,640]{1,0:T(8,128)(4,1)S(1)} %concatenate.6, bf16[32,640,576]{1,2,0:T(8,128)(2,1)} %constant_dynamic-update-slice_fusion, bf16[32,128,576]{2,1,0:T(8,128)(2,1)} %all-gather.2.cloned.1.call-done), kind=kOutput, calls=%fused_computation.5 | convolution fusion | flops 3027759104 | bytes 38834176 | tf_op jit(solution)/shard_map/rhw,rkw->rhk/dot_general | solution.py:31
  85.6 59.2 %pmax.7 = f32[32,128]{1,0:T(8,128)S(1)} all-reduce(f32[32,128]{1,0:T(8,128)S(1)} %get-tuple-element.7), channel_id=1, replica_groups=mesh['groups'=2,'seq'=16] {'seq'}, use_global_device_ids=true, to_apply=%region_4.5 | all-reduce | flops 4096 | bytes 32768 | tf_op jit(solution)/shard_map/pmax | solution.py:40
  144.8 0.0 copy-start.3
  144.8 0.0 copy-start.1
  144.8 16.3 %fusion = f32[32,128,512]{2,1,0:T(8,128)} fusion(bf16[32,640,576]{1,2,0:T(8,128)(2,1)} %constant_dynamic-update-slice_fusion, f32[32,640,128]{2,1,0:T(8,128)} %get-tuple-element.8, f32[32,128]{1,0:T(8,128)S(1)} %pmax.7, pred[32,640]{1,0:T(8,128)(4,1)S(1)} %concatenate.6), kind=kOutput, calls=%fused_computation.2 | convolution fusion | flops 2694840320 | bytes 39882752 | tf_op jit(solution)/shard_map/rhk,rkl->rhl/dot_general | solution.py:44
  161.1 0.0 reduce-scatter.3.cloned.1.call-update
  161.1 0.0 copy-done.3
  161.1 0.6 dynamic-slice
  162.3 9.0 %fusion.3 = f32[32,128]{1,0:T(8,128)S(1)} fusion(f32[32,640,128]{2,1,0:T(8,128)} %get-tuple-element.8, f32[32,128]{1,0:T(8,128)S(1)} %pmax.7, pred[32,640]{1,0:T(8,128)(4,1)S(1)} %concatenate.6), kind=kLoop, calls=%fused_computation.8 | loop fusion | flops 10481664 | bytes 10539008 | tf_op jit(solution)/shard_map/reduce_sum | solution.py:42
  171.4 60.6 %all-reduce.1 = f32[32,128]{1,0:T(8,128)S(1)} all-reduce(f32[32,128]{1,0:T(8,128)S(1)} %fusion.3), channel_id=3, replica_groups=mesh['groups'=2,'seq'=16] {'seq'}, use_global_device_ids=true, to_apply=%region_7.8.clone | all-reduce | flops 4096 | bytes 32768
  231.9 0.1 constant_dynamic-slice_fusion
  232.0 30.9 %reduce-scatter.3.cloned.1.call-done = f32[32,8,512]{2,1,0:T(8,128)} async-done(((f32[32,128,512]{2,1,0:T(8,128)}), f32[32,8,512]{2,1,0:T(8,128)}) %reduce-scatter.3.cloned.1.call-update) | async-done | bytes 524304 | tf_op jit(solution)/shard_map/reduce_scatter | solution.py:49
  262.9 1.9 divide_convert_fusion
  264.8 0.0 copy-done.1
  (7 shorter events, 0.1 us)
Async XLA Ops:
  6.5 4.0 %copy-start = (bf16[32,64,576]{2,1,0:T(8,128)(2,1)S(1)}, bf16[32,64,576]{2,1,0:T(8,128)(2,1)}, u32[]{:S(2)}) copy-start(bf16[32,64,576]{2,1,0:T(8,128)(2,1)} %param.7) | copy-start | bytes 7077892
  6.5 62.0 %all-gather.2.cloned.1.call-start = ((), (), s32[]{:S(2)}) async-start(), calls=%async_computation.1 | async-start | bytes 5570560 | tf_op jit(solution)/shard_map/all_gather | solution.py:33
  7.3 255.7 %reduce-scatter.3.cloned.1.call-start = ((), (), s32[]{:S(2)}) async-start(), calls=%async_computation.2 | async-start | bytes 8912896 | tf_op jit(solution)/shard_map/reduce_scatter | solution.py:49
  15.8 7.8 %copy-start.2 = (s32[32]{0:T(128)S(1)}, s32[32]{0:T(128)}, u32[]{:S(2)}) copy-start(s32[32]{0:T(128)} %param.11) | copy-start | bytes 388
  144.8 16.3 %copy-start.3 = (u32[32]{0:T(128)S(1)}, u32[32]{0:T(128)}, u32[]{:S(2)}) copy-start(u32[32]{0:T(128)} %constant.30) | copy-start | bytes 388
  144.8 120.0 %copy-start.1 = (bf16[32,64,576]{2,1,0:T(8,128)(2,1)S(1)}, bf16[32,64,576]{2,1,0:T(8,128)(2,1)}, u32[]{:S(2)}) copy-start(bf16[32,64,576]{2,1,0:T(8,128)(2,1)} %param.7) | copy-start | bytes 7077892
Sparse Core Ops, SparseCore 0:
  9.5 58.9 all-gather.1
  161.2 101.6 reduce-scatter.2
where the time goes:
time: 272 us
  blocking collectives  120 us (44%)
  waiting for transfers between devices  54.5 us (20%)
  local copies, waits for them, and re-layouts  35.7 us (13%)
  matrix products  33.4 us (12%)
  other arithmetic  14.1 us (5%)
  between operations  14.1 us (5%)
    unnamed x1, blocking collectives  60.6 us
    pmax x1, blocking collectives, body(): highest = lax.pmax(jnp.max(scores, axis=2), 'seq')  59.2 us
    reduce_scatter x1, waiting for transfers between devices, body(): lax.psum_scatter(weighted, 'seq', scatter_dimension=1, tiled=True)  30.9 us
    all_gather x1, waiting for transfers between devices, body(): lax.all_gather(queries, 'seq', axis=1, tiled=True)  22.9 us
    unnamed x11, local copies, waits for them, and re-layouts  17.6 us
    dot_general x1, matrix products, body(): jnp.einsum('rhw,rkw->rhk', lax.all_gather(queries, 'seq', axis=1, tiled=T...  17.1 us
    dot_general x1, matrix products, body(): jnp.einsum('rhk,rkl->rhl', rounded, request_keys[:, :, :LAT], preferred_e...  16.3 us
    reduce_sum x1, other arithmetic, body(): weight_sum = jnp.sum(weights, axis=2)  9.02 us
  transfers between devices with their start and end apart: 2, of which 2 were waited for; matrix products, arithmetic and copies ran while one was open for 18% of the time, Pallas kernels for 0%

commit v1 on v0

--- a/solution.py
+++ b/solution.py
@@ -1,6 +1,10 @@
+import functools
+
 import jax
 import jax.numpy as jnp
 from jax import lax
+from jax.experimental import pallas as pl
+from jax.experimental.pallas import tpu as pltpu
 from jax.sharding import PartitionSpec as P
 
 LAT = 512
@@ -51,9 +55,356 @@
     return (weighted / weight_sum[:, :, None]).astype(jnp.bfloat16)
 
 
+MESH = pl.DeviceIdType.MESH
+REQ_CHUNK = 4
+
+
+def kernel(
+    chips,
+    order_ref,
+    prefix_ref,
+    length_ref,
+    q_hbm,
+    pool_hbm,
+    suffix_hbm,
+    out_ref,
+    pool_v,
+    suffix_v,
+    q_v,
+    o_s,
+    stat_s,
+    o_r,
+    stat_r,
+    local_sem,
+    pool_sem,
+    suf_sem,
+    q_send,
+    q_recv,
+    o_send,
+    o_recv,
+    t_send,
+    t_recv,
+):
+    group = lax.axis_index("groups")
+    position = lax.axis_index("seq")
+    core = lax.rem(position, 2)
+    me = lax.div(position, 2)
+    column = lax.rem(me, 2)
+    depth = chips // 2
+    row = lax.div(me, 2)
+    partner = position + 1 - 2 * core
+    across = me + 1 - 2 * column
+
+    def device(chip):
+        return (group, chip * 2 + core)
+
+    def chip_at(step):
+        return lax.rem(me + step, chips)
+
+    def row_at(step):
+        return lax.rem(row + step, depth) * 2 + column
+
+    blocks = pool_hbm.shape[0]
+    requests = suffix_hbm.shape[0]
+    slots = suffix_hbm.shape[1]
+    pairs = q_hbm.shape[0]
+    heads = q_hbm.shape[1] // 2
+    chunks = requests // REQ_CHUNK
+    chunk_pairs = REQ_CHUNK // 2
+
+    barrier = pltpu.get_barrier_semaphore()
+    pl.semaphore_signal(barrier, inc=1, device_id=(group, partner), device_id_type=MESH)
+    for step in range(1, chips):
+        pl.semaphore_signal(
+            barrier, inc=1, device_id=device(chip_at(step)), device_id_type=MESH
+        )
+
+    def rows_of(c):
+        return pl.ds(c * chunk_pairs, chunk_pairs)
+
+    def reqs_of(c):
+        return pl.ds(c * REQ_CHUNK, REQ_CHUNK)
+
+    def q_local():
+        return pltpu.make_async_copy(q_hbm, q_v.at[me], local_sem.at[0])
+
+    def pool_local():
+        return pltpu.make_async_copy(pool_hbm, pool_v.at[core], local_sem.at[1])
+
+    def suffix_local(c):
+        return pltpu.make_async_copy(
+            suffix_hbm.at[reqs_of(c)], suffix_v.at[core, reqs_of(c)], local_sem.at[2 + c]
+        )
+
+    def q_copy(c, step):
+        dest = across if step == 0 else row_at(step)
+        return pltpu.make_async_remote_copy(
+            src_ref=q_hbm.at[rows_of(c)],
+            dst_ref=q_v.at[me, rows_of(c)],
+            send_sem=q_send.at[step, c],
+            recv_sem=q_recv.at[step, c],
+            device_id=device(dest),
+            device_id_type=MESH,
+        )
+
+    def q_forward(c, step):
+        source = row_at(depth - step)
+        return pltpu.make_async_remote_copy(
+            src_ref=q_v.at[source, rows_of(c)],
+            dst_ref=q_v.at[source, rows_of(c)],
+            send_sem=q_send.at[depth - 1 + step, c],
+            recv_sem=q_recv.at[depth - 1 + step, c],
+            device_id=device(across),
+            device_id_type=MESH,
+        )
+
+    def pool_remote():
+        return pltpu.make_async_remote_copy(
+            src_ref=pool_hbm,
+            dst_ref=pool_v.at[core],
+            send_sem=pool_sem.at[0],
+            recv_sem=pool_sem.at[1],
+            device_id=(group, partner),
+            device_id_type=MESH,
+        )
+
+    def suffix_remote(c):
+        return pltpu.make_async_remote_copy(
+            src_ref=suffix_hbm.at[reqs_of(c)],
+            dst_ref=suffix_v.at[core, reqs_of(c)],
+            send_sem=suf_sem.at[0, c],
+            recv_sem=suf_sem.at[1, c],
+            device_id=(group, partner),
+            device_id_type=MESH,
+        )
+
+    def o_copy(c, step):
+        dest = chip_at(step)
+        return pltpu.make_async_remote_copy(
+            src_ref=o_s.at[dest, rows_of(c)],
+            dst_ref=o_r.at[me, rows_of(c)],
+            send_sem=o_send.at[step, c],
+            recv_sem=o_recv.at[step, c],
+            device_id=device(dest),
+            device_id_type=MESH,
+        )
+
+    def t_copy(c, step):
+        dest = chip_at(step)
+        return pltpu.make_async_remote_copy(
+            src_ref=stat_s.at[dest, c],
+            dst_ref=stat_r.at[me, c],
+            send_sem=t_send.at[step, c],
+            recv_sem=t_recv.at[step, c],
+            device_id=device(dest),
+            device_id_type=MESH,
+        )
+
+    def o_local(c):
+        return pltpu.make_async_copy(
+            o_s.at[me, rows_of(c)], o_r.at[me, rows_of(c)], o_send.at[0, c]
+        )
+
+    def t_local(c):
+        return pltpu.make_async_copy(stat_s.at[me, c], stat_r.at[me, c], t_send.at[0, c])
+
+    def loop(count, body):
+        def step(c, carry):
+            body(c)
+            return carry
+
+        lax.fori_loop(0, count, step, 0)
+
+    q_local().start()
+    pool_local().start()
+    loop(chunks, lambda c: suffix_local(c).start())
+    pl.semaphore_wait(barrier, chips)
+
+    pool_remote().start()
+
+    def start_q(c):
+        for step in range(1, depth):
+            q_copy(c, step).start()
+        q_copy(c, 0).start()
+        suffix_remote(c).start()
+
+    loop(chunks, start_q)
+
+    def forward(c):
+        for step in range(1, depth):
+            q_copy(c, step).wait_recv()
+            q_forward(c, step).start()
+
+    forward(0)
+    q_local().wait()
+    pool_local().wait()
+    pool_remote().wait()
+
+    lanes = lax.broadcasted_iota(jnp.int32, (chips * heads, 128), 1)
+    slot_ids = lax.broadcasted_iota(jnp.int32, (1, 2 * slots), 1) + me * (2 * slots)
+    prefixes = order_ref.shape[1]
+    per_prefix = blocks // prefixes
+
+    def attend(q, request):
+        chosen = prefix_ref[request]
+        parts = []
+        for side in range(2):
+            for k in range(per_prefix):
+                parts.append(pool_v[side, order_ref[side * per_prefix + k, chosen]])
+        parts.append(suffix_v[0, request])
+        parts.append(suffix_v[1, request])
+        keys = jnp.concatenate(parts, axis=0)
+        scores = (
+            lax.dot_general(
+                q, keys, (((1,), (1,)), ((), ())), preferred_element_type=jnp.float32
+            )
+            * score_scale
+        )
+        split = keys.shape[0] - 2 * slots
+        live = slot_ids < length_ref[request]
+        scores = jnp.concatenate(
+            [scores[:, :split], jnp.where(live, scores[:, split:], -jnp.inf)], axis=1
+        )
+        highest = jnp.max(scores, axis=1, keepdims=True)
+        weights = jnp.exp(scores - highest)
+        total = jnp.sum(weights, axis=1, keepdims=True)
+        mixed = jnp.dot(
+            weights.astype(jnp.bfloat16), keys[:, :LAT], preferred_element_type=jnp.float32
+        )
+        return mixed / total, highest, total
+
+    def do_chunk(c):
+        @pl.when(c + 1 < chunks)
+        def _():
+            forward(c + 1)
+
+        q_copy(c, 0).wait_recv()
+        for step in range(1, depth):
+            q_forward(c, step).wait_recv()
+        suffix_local(c).wait()
+        suffix_remote(c).wait()
+        stats = jnp.zeros((chips * heads, 128), jnp.float32)
+        for half in range(chunk_pairs):
+            pair = c * chunk_pairs + half
+            q = q_v[:, pair].astype(jnp.float32).reshape(chips, 2, heads, q_v.shape[-1])
+            outs = []
+            for i in range(2):
+                request = pair * 2 + i
+                one = q[:, i].reshape(chips * heads, q_v.shape[-1]).astype(jnp.bfloat16)
+                mixed, highest, total = attend(one, request)
+                at = 2 * (half * 2 + i)
+                stats = jnp.where(lanes == at, highest, stats)
+                stats = jnp.where(lanes == at + 1, total, stats)
+                outs.append(mixed.reshape(chips, heads, LAT))
+            both = jnp.concatenate(outs, axis=1)
+            o_s[:, pair] = both.astype(jnp.bfloat16)
+        stat_s[:, c] = stats.reshape(chips, heads, 128)
+        for step in range(1, chips):
+            o_copy(c, step).start()
+            t_copy(c, step).start()
+        o_local(c).start()
+        t_local(c).start()
+
+    loop(chunks, do_chunk)
+
+    def finish(c):
+        o_local(c).wait()
+        t_local(c).wait()
+        for step in range(1, chips):
+            o_copy(c, step).wait_recv()
+            t_copy(c, step).wait_recv()
+        stats = stat_r[:, c]
+        for half in range(chunk_pairs):
+            pair = c * chunk_pairs + half
+            both = o_r[:, pair].astype(jnp.float32)
+            outs = []
+            for i in range(2):
+                at = 2 * (half * 2 + i)
+                top = stats[:, :, at : at + 1]
+                share = jnp.exp(top - jnp.max(top, axis=0, keepdims=True)) * stats[:, :, at + 1 : at + 2]
+                share = share / jnp.sum(share, axis=0, keepdims=True)
+                outs.append(jnp.sum(both[:, i * heads : (i + 1) * heads] * share, axis=0))
+            out_ref[pair] = jnp.concatenate(outs, axis=0).astype(jnp.bfloat16)
+
+    loop(chunks, finish)
+
+    def drain(c):
+        for step in range(depth):
+            q_copy(c, step).wait_send()
+        for step in range(1, depth):
+            q_forward(c, step).wait_send()
+        for step in range(1, chips):
+            o_copy(c, step).wait_send()
+            t_copy(c, step).wait_send()
+
+    loop(chunks, drain)
+
+
+def fused_body(seq, queries, prefix_pool, block_table, prefix_of, suffix_cache, suffix_len):
+    blocks_here, block_rows, channels = prefix_pool.shape
+    prefix_total = block_table.shape[0]
+    requests, heads, _ = queries.shape
+    slots = suffix_cache.shape[1]
+    per_prefix = blocks_here // prefix_total
+    chips = seq // 2
+    chunks = requests // REQ_CHUNK
+    pairs = requests // 2
+    chip = lax.axis_index("seq") // 2
+
+    sides = chip * 2 + lax.iota(jnp.int32, 2)
+    here = (block_table // blocks_here)[None] == sides[:, None, None]
+    before = jnp.tril(jnp.ones((block_table.shape[1],) * 2, jnp.int32), -1)
+    rank = jnp.sum(here[:, :, None, :] * before, axis=3)
+    pick = here[:, None] & (rank[:, None] == lax.iota(jnp.int32, per_prefix)[None, :, None, None])
+    local = block_table - block_table // blocks_here * blocks_here
+    order = jnp.sum(jnp.where(pick, local[None, None], 0), axis=3).reshape(2 * per_prefix, prefix_total)
+
+    any_spec = pl.BlockSpec(memory_space=pltpu.HBM)
+    smem = pl.BlockSpec(memory_space=pltpu.SMEM)
+    dma = pltpu.SemaphoreType.DMA
+    out = pl.pallas_call(
+        functools.partial(kernel, chips),
+        out_shape=jax.ShapeDtypeStruct((pairs, 2 * heads, LAT), jnp.bfloat16),
+        in_specs=[smem, smem, smem, any_spec, any_spec, any_spec],
+        out_specs=pl.BlockSpec(memory_space=pltpu.VMEM),
+        scratch_shapes=[
+            pltpu.VMEM((2, blocks_here, block_rows, channels), jnp.bfloat16),
+            pltpu.VMEM((2, requests, slots, channels), jnp.bfloat16),
+            pltpu.VMEM((chips, pairs, 2 * heads, channels), jnp.bfloat16),
+            pltpu.VMEM((chips, pairs, 2 * heads, LAT), jnp.bfloat16),
+            pltpu.VMEM((chips, chunks, heads, 128), jnp.float32),
+            pltpu.VMEM((chips, pairs, 2 * heads, LAT), jnp.bfloat16),
+            pltpu.VMEM((chips, chunks, heads, 128), jnp.float32),
+            dma((2 + chunks,)),
+            dma((2,)),
+            dma((2, chunks)),
+            dma((chips, chunks)),
+            dma((chips, chunks)),
+            dma((chips, chunks)),
+            dma((chips, chunks)),
+            dma((chips, chunks)),
+            dma((chips, chunks)),
+        ],
+        compiler_params=pltpu.CompilerParams(
+            collective_id=0, has_side_effects=True, vmem_limit_bytes=50 * 1024 * 1024
+        ),
+    )(
+        order,
+        prefix_of,
+        suffix_len,
+        queries.reshape(pairs, 2 * heads, channels),
+        prefix_pool,
+        suffix_cache,
+    )
+    return out.reshape(requests, heads, LAT)
+
+
 def solution(mesh):
+    seq = mesh.shape["seq"]
+    wide = seq == 16
+    local = functools.partial(fused_body, seq) if wide else body
     return jax.shard_map(
-        body,
+        local,
         mesh=mesh,
         in_specs=(
             P("groups", "seq", None),

time: 272 us -> 98.9 us (0.36)
  blocking collectives: 120 us -> 0 us
  Pallas kernels: 0 us -> 88.7 us
  waiting for transfers between devices: 54.5 us -> 0 us
  matrix products: 33.4 us -> 0 us
  local copies, waits for them, and re-layouts: 35.7 us -> 8.63 us
  between operations: 14.1 us -> 0.04 us
  other arithmetic: 14.1 us -> 1.29 us
    pallas_call x0 -> x1, Pallas kernels: none -> 88.7 us  [fused_body(): pl.pallas_call(functools.partial(kernel, chips), out_shape=jax.ShapeDtype...]
    unnamed x1 -> x0, blocking collectives: 60.6 us -> none
    pmax x1 -> x0, blocking collectives: 59.2 us -> none  [body(): highest = lax.pmax(jnp.max(scores, axis=2), 'seq')]
    dot_general x2 -> x0, matrix products: 33.4 us -> none  [the longest x1 17.1 us: body(): jnp.einsum('rhw,rkw->rhk', lax.all_gather(queries, 'seq', axis=1, tiled=T...]
    reduce_scatter x1 -> x0, waiting for transfers between devices: 30.9 us -> none  [body(): lax.psum_scatter(weighted, 'seq', scatter_dimension=1, tiled=True)]
    all_gather x1 -> x0, waiting for transfers between devices: 22.9 us -> none  [body(): lax.all_gather(queries, 'seq', axis=1, tiled=True)]
    gather x2 -> x0, local copies, waits for them, and re-layouts: 10.2 us -> none  [the longest x1 7.83 us: body(): request_keys = jnp.concatenate([segments[prefix_of], suffix_cache], axis=1)]
    unnamed x11 -> x10, local copies, waits for them, and re-layouts: 17.6 us -> 8.54 us
  transfers between devices with their start and end apart: 2 -> 0, of which waited for: 2 -> 0; matrix products, arithmetic and copies ran while one was open for 18% -> 0% of each run, Pallas kernels for 0% -> 0%
where the time goes in v1:
time: 98.9 us; the launch traced here: 98.7 us
  Pallas kernels  88.7 us (90%)
  local copies, waits for them, and re-layouts  8.63 us (9%)
  other arithmetic  1.29 us (1%)
    pallas_call x1, Pallas kernels, fused_body(): pl.pallas_call(functools.partial(kernel, chips), out_shape=jax.ShapeDtype...  88.7 us
    unnamed x10, local copies, waits for them, and re-layouts  8.54 us

profile of v1, /device:TPU:0, one launch (start us, length us, event | category | flops | bytes accessed | tf_op | source)
XLA Modules:
  0.0 98.7 jit_solution(8371920037201647811)
XLA Ops:
  0.0 0.7 add_select_fusion
  0.7 0.1 fusion.4
  0.8 0.1 fusion
  0.9 0.2 multiply_reduce_fusion
  1.1 0.2 select_reduce_fusion
  1.3 0.1 copy.12
  1.4 0.0 copy-start
  1.4 0.0 copy-start.1
  1.4 0.0 copy-start.2
  1.4 0.0 copy-start.3
  1.4 7.8 %copy.11.suffix_hbm = bf16[32,128,576]{2,1,0:T(8,128)(2,1)} copy(bf16[32,128,576]{1,2,0:T(8,128)(2,1)} %param.10) | data formatting | bytes 9437184 | tf_op args[4]
  9.2 0.0 copy-done
  9.2 0.0 copy-done.1
  9.2 0.0 copy-done.2
  9.2 0.0 copy-done.3
  9.2 88.7 %shard_map.64 = bf16[16,16,512]{2,1,0:T(8,128)(2,1)S(1)} custom-call(s32[16,4]{1,0:T(8,128)S(1)} %bitcast.5, s32[32]{0:T(128)S(1)} %copy-done.2, s32[32]{0:T(128)S(1)} %copy-done.3, bf16[16,16,576]{2,1,0:T(8,128)(2,1)S(1)} %bitcast.4, bf16[32,64,576]{2,1,0:T(8,128)(2,1)S(1)} %copy-done, bf16[32,128,576]{2,1,0:T(8,128)(2,1)} %copy.11.suffix_hbm), custom_call_target="tpu_custom_call" | custom-call | tf_op jit(solution)/shard_map/pallas_call | solution.py:365
  98.0 0.7 copy.15
  (2 shorter events, 0.0 us)
Async XLA Ops:
  1.4 7.8 %copy-start = (bf16[32,64,576]{2,1,0:T(8,128)(2,1)S(1)}, bf16[32,64,576]{2,1,0:T(8,128)(2,1)}, u32[]{:S(2)}) copy-start(bf16[32,64,576]{2,1,0:T(8,128)(2,1)} %pool_hbm.1) | copy-start | bytes 7077892
  1.4 7.8 %copy-start.1 = (bf16[32,8,576]{2,1,0:T(8,128)(2,1)S(1)}, bf16[32,8,576]{2,1,0:T(8,128)(2,1)}, u32[]{:S(2)}) copy-start(bf16[32,8,576]{2,1,0:T(8,128)(2,1)} %param.6) | copy-start | bytes 884740
  1.4 7.8 %copy-start.2 = (s32[32]{0:T(128)S(1)}, s32[32]{0:T(128)}, u32[]{:S(2)}) copy-start(s32[32]{0:T(128)} %prefix_ref.1) | copy-start | bytes 388
  1.4 7.8 %copy-start.3 = (s32[32]{0:T(128)S(1)}, s32[32]{0:T(128)}, u32[]{:S(2)}) copy-start(s32[32]{0:T(128)} %length_ref.1) | copy-start | bytes 388

commit v2 on v1

--- a/solution.py
+++ b/solution.py
@@ -57,6 +57,7 @@
 
 MESH = pl.DeviceIdType.MESH
 REQ_CHUNK = 4
+LAG = 2
 
 
 def kernel(
@@ -71,19 +72,23 @@
     pool_v,
     suffix_v,
     q_v,
-    o_s,
-    stat_s,
-    o_r,
-    stat_r,
+    kept_v,
+    kept_stat,
+    y_s,
+    ystat_s,
+    y_r,
+    ystat_r,
+    z_s,
+    zstat_s,
+    z_r,
+    zstat_r,
     local_sem,
     pool_sem,
     suf_sem,
     q_send,
     q_recv,
-    o_send,
-    o_recv,
-    t_send,
-    t_recv,
+    y_sem,
+    z_sem,
 ):
     group = lax.axis_index("groups")
     position = lax.axis_index("seq")
@@ -106,7 +111,7 @@
 
     blocks = pool_hbm.shape[0]
     requests = suffix_hbm.shape[0]
-    slots = suffix_hbm.shape[1]
+    slots = suffix_hbm.shape[2]
     pairs = q_hbm.shape[0]
     heads = q_hbm.shape[1] // 2
     chunks = requests // REQ_CHUNK
@@ -126,7 +131,7 @@
         return pl.ds(c * REQ_CHUNK, REQ_CHUNK)
 
     def q_local():
-        return pltpu.make_async_copy(q_hbm, q_v.at[me], local_sem.at[0])
+        return pltpu.make_async_copy(q_hbm, q_v.at[0, row], local_sem.at[0])
 
     def pool_local():
         return pltpu.make_async_copy(pool_hbm, pool_v.at[core], local_sem.at[1])
@@ -140,7 +145,7 @@
         dest = across if step == 0 else row_at(step)
         return pltpu.make_async_remote_copy(
             src_ref=q_hbm.at[rows_of(c)],
-            dst_ref=q_v.at[me, rows_of(c)],
+            dst_ref=q_v.at[1 if step == 0 else 0, row, rows_of(c)],
             send_sem=q_send.at[step, c],
             recv_sem=q_recv.at[step, c],
             device_id=device(dest),
@@ -148,10 +153,10 @@
         )
 
     def q_forward(c, step):
-        source = row_at(depth - step)
-        return pltpu.make_async_remote_copy(
-            src_ref=q_v.at[source, rows_of(c)],
-            dst_ref=q_v.at[source, rows_of(c)],
+        source = lax.rem(row + depth - step, depth)
+        return pltpu.make_async_remote_copy(
+            src_ref=q_v.at[0, source, rows_of(c)],
+            dst_ref=q_v.at[1, source, rows_of(c)],
             send_sem=q_send.at[depth - 1 + step, c],
             recv_sem=q_recv.at[depth - 1 + step, c],
             device_id=device(across),
@@ -178,35 +183,47 @@
             device_id_type=MESH,
         )
 
-    def o_copy(c, step):
-        dest = chip_at(step)
-        return pltpu.make_async_remote_copy(
-            src_ref=o_s.at[dest, rows_of(c)],
-            dst_ref=o_r.at[me, rows_of(c)],
-            send_sem=o_send.at[step, c],
-            recv_sem=o_recv.at[step, c],
-            device_id=device(dest),
-            device_id_type=MESH,
-        )
-
-    def t_copy(c, step):
-        dest = chip_at(step)
-        return pltpu.make_async_remote_copy(
-            src_ref=stat_s.at[dest, c],
-            dst_ref=stat_r.at[me, c],
-            send_sem=t_send.at[step, c],
-            recv_sem=t_recv.at[step, c],
-            device_id=device(dest),
-            device_id_type=MESH,
-        )
-
-    def o_local(c):
-        return pltpu.make_async_copy(
-            o_s.at[me, rows_of(c)], o_r.at[me, rows_of(c)], o_send.at[0, c]
-        )
-
-    def t_local(c):
-        return pltpu.make_async_copy(stat_s.at[me, c], stat_r.at[me, c], t_send.at[0, c])
+    def y_copy(c):
+        return pltpu.make_async_remote_copy(
+            src_ref=y_s.at[:, rows_of(c)],
+            dst_ref=y_r.at[:, rows_of(c)],
+            send_sem=y_sem.at[0, c],
+            recv_sem=y_sem.at[1, c],
+            device_id=device(across),
+            device_id_type=MESH,
+        )
+
+    def ystat_copy(c):
+        return pltpu.make_async_remote_copy(
+            src_ref=ystat_s.at[c],
+            dst_ref=ystat_r.at[c],
+            send_sem=y_sem.at[2, c],
+            recv_sem=y_sem.at[3, c],
+            device_id=device(across),
+            device_id_type=MESH,
+        )
+
+    def z_copy(c, step):
+        dest = lax.rem(row + step, depth)
+        return pltpu.make_async_remote_copy(
+            src_ref=z_s.at[dest, rows_of(c)],
+            dst_ref=z_r.at[row, rows_of(c)],
+            send_sem=z_sem.at[0, step - 1, c],
+            recv_sem=z_sem.at[1, step - 1, c],
+            device_id=device(row_at(step)),
+            device_id_type=MESH,
+        )
+
+    def zstat_copy(c, step):
+        dest = lax.rem(row + step, depth)
+        return pltpu.make_async_remote_copy(
+            src_ref=zstat_s.at[dest, c],
+            dst_ref=zstat_r.at[row, c],
+            send_sem=z_sem.at[2, step - 1, c],
+            recv_sem=z_sem.at[3, step - 1, c],
+            device_id=device(row_at(step)),
+            device_id_type=MESH,
+        )
 
     def loop(count, body):
         def step(c, carry):
@@ -220,15 +237,19 @@
     loop(chunks, lambda c: suffix_local(c).start())
     pl.semaphore_wait(barrier, chips)
 
-    pool_remote().start()
-
     def start_q(c):
         for step in range(1, depth):
             q_copy(c, step).start()
         q_copy(c, 0).start()
         suffix_remote(c).start()
 
-    loop(chunks, start_q)
+    start_q(0)
+    pool_remote().start()
+
+    def start_later(c):
+        start_q(c + 1)
+
+    loop(chunks - 1, start_later)
 
     def forward(c):
         for step in range(1, depth):
@@ -240,7 +261,8 @@
     pool_local().wait()
     pool_remote().wait()
 
-    lanes = lax.broadcasted_iota(jnp.int32, (chips * heads, 128), 1)
+    lanes = lax.broadcasted_iota(jnp.int32, (heads, 128), 1)
+    half_rows = depth * heads
     slot_ids = lax.broadcasted_iota(jnp.int32, (1, 2 * slots), 1) + me * (2 * slots)
     prefixes = order_ref.shape[1]
     per_prefix = blocks // prefixes
@@ -251,25 +273,32 @@
         for side in range(2):
             for k in range(per_prefix):
                 parts.append(pool_v[side, order_ref[side * per_prefix + k, chosen]])
-        parts.append(suffix_v[0, request])
-        parts.append(suffix_v[1, request])
         keys = jnp.concatenate(parts, axis=0)
-        scores = (
-            lax.dot_general(
-                q, keys, (((1,), (1,)), ((), ())), preferred_element_type=jnp.float32
-            )
-            * score_scale
-        )
-        split = keys.shape[0] - 2 * slots
+        tails = jnp.concatenate([suffix_v[0, request], suffix_v[1, request]], axis=1)
+        prefix_scores = lax.dot_general(
+            q, keys, (((1,), (1,)), ((), ())), preferred_element_type=jnp.float32
+        )
+        suffix_scores = jnp.dot(q, tails, preferred_element_type=jnp.float32)
         live = slot_ids < length_ref[request]
         scores = jnp.concatenate(
-            [scores[:, :split], jnp.where(live, scores[:, split:], -jnp.inf)], axis=1
+            [
+                prefix_scores * score_scale,
+                jnp.where(live, suffix_scores * score_scale, -jnp.inf),
+            ],
+            axis=1,
         )
         highest = jnp.max(scores, axis=1, keepdims=True)
         weights = jnp.exp(scores - highest)
         total = jnp.sum(weights, axis=1, keepdims=True)
+        rounded = weights.astype(jnp.bfloat16)
+        split = keys.shape[0]
         mixed = jnp.dot(
-            weights.astype(jnp.bfloat16), keys[:, :LAT], preferred_element_type=jnp.float32
+            rounded[:, :split], keys[:, :LAT], preferred_element_type=jnp.float32
+        ) + lax.dot_general(
+            rounded[:, split:],
+            tails[:LAT],
+            (((1,), (1,)), ((), ())),
+            preferred_element_type=jnp.float32,
         )
         return mixed / total, highest, total
 
@@ -283,47 +312,101 @@
             q_forward(c, step).wait_recv()
         suffix_local(c).wait()
         suffix_remote(c).wait()
-        stats = jnp.zeros((chips * heads, 128), jnp.float32)
+        kept = jnp.zeros((heads, 128), jnp.float32)
+        sent = jnp.zeros((heads, 128), jnp.float32)
         for half in range(chunk_pairs):
             pair = c * chunk_pairs + half
-            q = q_v[:, pair].astype(jnp.float32).reshape(chips, 2, heads, q_v.shape[-1])
+            q = q_v[:, :, pair].astype(jnp.float32).reshape(chips, 2, heads, q_v.shape[-1])
             outs = []
             for i in range(2):
-                request = pair * 2 + i
                 one = q[:, i].reshape(chips * heads, q_v.shape[-1]).astype(jnp.bfloat16)
-                mixed, highest, total = attend(one, request)
-                at = 2 * (half * 2 + i)
-                stats = jnp.where(lanes == at, highest, stats)
-                stats = jnp.where(lanes == at + 1, total, stats)
-                outs.append(mixed.reshape(chips, heads, LAT))
-            both = jnp.concatenate(outs, axis=1)
-            o_s[:, pair] = both.astype(jnp.bfloat16)
-        stat_s[:, c] = stats.reshape(chips, heads, 128)
-        for step in range(1, chips):
-            o_copy(c, step).start()
-            t_copy(c, step).start()
-        o_local(c).start()
-        t_local(c).start()
-
-    loop(chunks, do_chunk)
+                mixed, highest, total = attend(one, pair * 2 + i)
+                for z in range(depth):
+                    at = 2 * (z * REQ_CHUNK + half * 2 + i)
+                    low = slice(z * heads, (z + 1) * heads)
+                    high = slice(half_rows + z * heads, half_rows + (z + 1) * heads)
+                    kept = jnp.where(lanes == at, highest[low], kept)
+                    kept = jnp.where(lanes == at + 1, total[low], kept)
+                    sent = jnp.where(lanes == at, highest[high], sent)
+                    sent = jnp.where(lanes == at + 1, total[high], sent)
+                outs.append(mixed.reshape(2, depth, heads, LAT))
+            kept_v[:, pair] = jnp.concatenate([outs[0][0], outs[1][0]], axis=1)
+            y_s[:, pair] = jnp.concatenate([outs[0][1], outs[1][1]], axis=1).astype(jnp.bfloat16)
+        kept_stat[c] = kept
+        ystat_s[c] = sent
+        y_copy(c).start()
+        ystat_copy(c).start()
+
+    def merge_columns(c):
+        y_copy(c).wait_recv()
+        ystat_copy(c).wait_recv()
+        ours = kept_stat[c]
+        theirs = ystat_r[c]
+        for z in range(depth):
+            stats = jnp.zeros((heads, 128), jnp.float32)
+            for half in range(chunk_pairs):
+                pair = c * chunk_pairs + half
+                mine = kept_v[z, pair]
+                other = y_r[z, pair].astype(jnp.float32)
+                outs = []
+                for i in range(2):
+                    at = 2 * (z * REQ_CHUNK + half * 2 + i)
+                    top_a = ours[:, at : at + 1]
+                    top_b = theirs[:, at : at + 1]
+                    top = jnp.maximum(top_a, top_b)
+                    part_a = jnp.exp(top_a - top) * ours[:, at + 1 : at + 2]
+                    part_b = jnp.exp(top_b - top) * theirs[:, at + 1 : at + 2]
+                    total = part_a + part_b
+                    low = slice(i * heads, (i + 1) * heads)
+                    outs.append(mine[low] * (part_a / total) + other[low] * (part_b / total))
+                    to = 2 * (half * 2 + i)
+                    stats = jnp.where(lanes == to, top, stats)
+                    stats = jnp.where(lanes == to + 1, total, stats)
+                both = jnp.concatenate(outs, axis=0)
+                kept_v[z, pair] = both
+                z_s[z, pair] = both.astype(jnp.bfloat16)
+            zstat_s[z, c] = stats
+        for step in range(1, depth):
+            z_copy(c, step).start()
+            zstat_copy(c, step).start()
+
+    def stage(c):
+        @pl.when(c < chunks)
+        def _():
+            do_chunk(c)
+
+        @pl.when(c >= LAG)
+        def _():
+            merge_columns(c - LAG)
+
+    loop(chunks + LAG, stage)
 
     def finish(c):
-        o_local(c).wait()
-        t_local(c).wait()
-        for step in range(1, chips):
-            o_copy(c, step).wait_recv()
-            t_copy(c, step).wait_recv()
-        stats = stat_r[:, c]
+        stats = [zstat_s[row, c]]
+        for step in range(1, depth):
+            z_copy(c, step).wait_recv()
+            zstat_copy(c, step).wait_recv()
+            stats.append(zstat_r[lax.rem(row + depth - step, depth), c])
         for half in range(chunk_pairs):
             pair = c * chunk_pairs + half
-            both = o_r[:, pair].astype(jnp.float32)
+            both = [kept_v[row, pair]]
+            for step in range(1, depth):
+                both.append(z_r[lax.rem(row + depth - step, depth), pair].astype(jnp.float32))
             outs = []
             for i in range(2):
                 at = 2 * (half * 2 + i)
-                top = stats[:, :, at : at + 1]
-                share = jnp.exp(top - jnp.max(top, axis=0, keepdims=True)) * stats[:, :, at + 1 : at + 2]
-                share = share / jnp.sum(share, axis=0, keepdims=True)
-                outs.append(jnp.sum(both[:, i * heads : (i + 1) * heads] * share, axis=0))
+                tops = [s[:, at : at + 1] for s in stats]
+                top = functools.reduce(jnp.maximum, tops)
+                shares = [
+                    jnp.exp(t - top) * s[:, at + 1 : at + 2] for t, s in zip(tops, stats)
+                ]
+                total = functools.reduce(jnp.add, shares)
+                low = slice(i * heads, (i + 1) * heads)
+                outs.append(
+                    functools.reduce(
+                        jnp.add, [b[low] * (s / total) for b, s in zip(both, shares)]
+                    )
+                )
             out_ref[pair] = jnp.concatenate(outs, axis=0).astype(jnp.bfloat16)
 
     loop(chunks, finish)
@@ -333,9 +416,11 @@
             q_copy(c, step).wait_send()
         for step in range(1, depth):
             q_forward(c, step).wait_send()
-        for step in range(1, chips):
-            o_copy(c, step).wait_send()
-            t_copy(c, step).wait_send()
+        y_copy(c).wait_send()
+        ystat_copy(c).wait_send()
+        for step in range(1, depth):
+            z_copy(c, step).wait_send()
+            zstat_copy(c, step).wait_send()
 
     loop(chunks, drain)
 
@@ -347,6 +432,7 @@
     slots = suffix_cache.shape[1]
     per_prefix = blocks_here // prefix_total
     chips = seq // 2
+    depth = chips // 2
     chunks = requests // REQ_CHUNK
     pairs = requests // 2
     chip = lax.axis_index("seq") // 2
@@ -369,24 +455,28 @@
         out_specs=pl.BlockSpec(memory_space=pltpu.VMEM),
         scratch_shapes=[
             pltpu.VMEM((2, blocks_here, block_rows, channels), jnp.bfloat16),
-            pltpu.VMEM((2, requests, slots, channels), jnp.bfloat16),
-            pltpu.VMEM((chips, pairs, 2 * heads, channels), jnp.bfloat16),
-            pltpu.VMEM((chips, pairs, 2 * heads, LAT), jnp.bfloat16),
-            pltpu.VMEM((chips, chunks, heads, 128), jnp.float32),
-            pltpu.VMEM((chips, pairs, 2 * heads, LAT), jnp.bfloat16),
-            pltpu.VMEM((chips, chunks, heads, 128), jnp.float32),
+            pltpu.VMEM((2, requests, channels, slots), jnp.bfloat16),
+            pltpu.VMEM((2, depth, pairs, 2 * heads, channels), jnp.bfloat16),
+            pltpu.VMEM((depth, pairs, 2 * heads, LAT), jnp.float32),
+            pltpu.VMEM((chunks, heads, 128), jnp.float32),
+            pltpu.VMEM((depth, pairs, 2 * heads, LAT), jnp.bfloat16),
+            pltpu.VMEM((chunks, heads, 128), jnp.float32),
+            pltpu.VMEM((depth, pairs, 2 * heads, LAT), jnp.bfloat16),
+            pltpu.VMEM((chunks, heads, 128), jnp.float32),
+            pltpu.VMEM((depth, pairs, 2 * heads, LAT), jnp.bfloat16),
+            pltpu.VMEM((depth, chunks, heads, 128), jnp.float32),
+            pltpu.VMEM((depth, pairs, 2 * heads, LAT), jnp.bfloat16),
+            pltpu.VMEM((depth, chunks, heads, 128), jnp.float32),
             dma((2 + chunks,)),
             dma((2,)),
             dma((2, chunks)),
             dma((chips, chunks)),
             dma((chips, chunks)),
-            dma((chips, chunks)),
-            dma((chips, chunks)),
-            dma((chips, chunks)),
-            dma((chips, chunks)),
+            dma((4, chunks)),
+            dma((4, depth - 1, chunks)),
         ],
         compiler_params=pltpu.CompilerParams(
-            collective_id=0, has_side_effects=True, vmem_limit_bytes=50 * 1024 * 1024
+            collective_id=0, has_side_effects=True, vmem_limit_bytes=63 * 1024 * 1024
         ),
     )(
         order,
@@ -394,7 +484,7 @@
         suffix_len,
         queries.reshape(pairs, 2 * heads, channels),
         prefix_pool,
-        suffix_cache,
+        jnp.swapaxes(suffix_cache, 1, 2),
     )
     return out.reshape(requests, heads, LAT)
 

time: 98.9 us -> 77.7 us (0.79)
  Pallas kernels: 88.7 us -> 73.9 us
  local copies, waits for them, and re-layouts: 8.63 us -> 2.37 us
    pallas_call x1, Pallas kernels: 88.7 us -> 73.9 us  [fused_body(): pl.pallas_call(functools.partial(kernel, chips), out_shape=jax.ShapeDtype...]
    unnamed x10 -> x1, local copies, waits for them, and re-layouts: 8.54 us -> 1.67 us
where the time goes in v2:
time: 77.7 us; the launch traced here: 77.5 us
  Pallas kernels  73.9 us (95%)
  local copies, waits for them, and re-layouts  2.37 us (3%)
  other arithmetic  1.29 us (2%)
    pallas_call x1, Pallas kernels, fused_body(): pl.pallas_call(functools.partial(kernel, chips), out_shape=jax.ShapeDtype...  73.9 us
    unnamed x1, local copies, waits for them, and re-layouts  1.67 us

profile of v2, /device:TPU:0, one launch (start us, length us, event | category | flops | bytes accessed | tf_op | source)
XLA Modules:
  0.0 77.5 jit_solution(5977800046974363852)
XLA Ops:
  0.0 0.7 add_select_fusion
  0.7 0.1 fusion.4
  0.8 0.1 fusion
  0.9 0.2 multiply_reduce_fusion
  1.1 0.2 select_reduce_fusion
  1.3 0.7 copy.10
  2.0 73.9 %shard_map.64 = bf16[16,16,512]{2,1,0:T(8,128)(2,1)} custom-call(s32[16,4]{1,0:T(8,128)} %bitcast.7, s32[32]{0:T(128)} %prefix_ref.1, s32[32]{0:T(128)} %length_ref.1, bf16[16,16,576]{2,1,0:T(8,128)(2,1)} %bitcast.6, bf16[32,64,576]{2,1,0:T(8,128)(2,1)} %pool_hbm.1, bf16[32,576,128]{2,1,0:T(8,128)(2,1)} %bitcast.4), custom_call_target="tpu_custom_call" | custom-call | tf_op jit(solution)/shard_map/pallas_call | solution.py:451
  75.9 1.7 %copy.13 = bf16[32,8,512]{2,1,0:T(8,128)(2,1)} copy(bf16[32,8,512]{2,1,0:T(8,128)(2,1)} %bitcast.5) | data formatting | bytes 524288
  (2 shorter events, 0.0 us)

commit v3 on v2

--- a/solution.py
+++ b/solution.py
@@ -99,6 +99,7 @@
     row = lax.div(me, 2)
     partner = position + 1 - 2 * core
     across = me + 1 - 2 * column
+    twin = row + 1 - 2 * lax.rem(row, 2)
 
     def device(chip):
         return (group, chip * 2 + core)
@@ -141,27 +142,31 @@
             suffix_hbm.at[reqs_of(c)], suffix_v.at[core, reqs_of(c)], local_sem.at[2 + c]
         )
 
-    def q_copy(c, step):
-        dest = across if step == 0 else row_at(step)
-        return pltpu.make_async_remote_copy(
-            src_ref=q_hbm.at[rows_of(c)],
-            dst_ref=q_v.at[1 if step == 0 else 0, row, rows_of(c)],
-            send_sem=q_send.at[step, c],
-            recv_sem=q_recv.at[step, c],
+    def q_move(c, side, source, kind, dest, to_side, fresh=False):
+        held = q_hbm.at[rows_of(c)] if fresh else q_v.at[side, source, rows_of(c)]
+        return pltpu.make_async_remote_copy(
+            src_ref=held,
+            dst_ref=q_v.at[to_side, source, rows_of(c)],
+            send_sem=q_send.at[kind, c],
+            recv_sem=q_recv.at[to_side * depth + source, c],
             device_id=device(dest),
             device_id_type=MESH,
         )
 
-    def q_forward(c, step):
-        source = lax.rem(row + depth - step, depth)
-        return pltpu.make_async_remote_copy(
-            src_ref=q_v.at[0, source, rows_of(c)],
-            dst_ref=q_v.at[1, source, rows_of(c)],
-            send_sem=q_send.at[depth - 1 + step, c],
-            recv_sem=q_recv.at[depth - 1 + step, c],
-            device_id=device(across),
-            device_id_type=MESH,
-        )
+    def q_up(c, source, fresh=False):
+        return q_move(c, 0, source, source, me + 2, 0, fresh)
+
+    def q_down(c, source, fresh=False):
+        return q_move(c, 0, source, depth + source, me - 2, 0, fresh)
+
+    def q_across(c, source, fresh=False):
+        return q_move(c, 0, source, 2 * depth + source, across, 1, fresh)
+
+    def q_swap(c):
+        return q_move(c, 1, row, 3 * depth, twin * 2 + column, 1)
+
+    def q_arrival(c, side, source):
+        return q_move(c, side, source, 0, across, side)
 
     def pool_remote():
         return pltpu.make_async_remote_copy(
@@ -238,10 +243,55 @@
     pl.semaphore_wait(barrier, chips)
 
     def start_q(c):
-        for step in range(1, depth):
-            q_copy(c, step).start()
-        q_copy(c, 0).start()
+        q_across(c, row, True).start()
+
+        @pl.when(row + 1 < depth)
+        def _():
+            q_up(c, row, True).start()
+
+        @pl.when(row > 0)
+        def _():
+            q_down(c, row, True).start()
+
         suffix_remote(c).start()
+
+    def relay(c, distance):
+        below, above = row - distance, row + distance
+
+        @pl.when(below >= 0)
+        def _():
+            q_arrival(c, 0, below).wait_recv()
+
+            @pl.when(row + 1 < depth)
+            def _():
+                q_up(c, below).start()
+
+            @pl.when(below != twin)
+            def _():
+                q_across(c, below).start()
+
+        @pl.when(above < depth)
+        def _():
+            q_arrival(c, 0, above).wait_recv()
+
+            @pl.when(row > 0)
+            def _():
+                q_down(c, above).start()
+
+            @pl.when(above != twin)
+            def _():
+                q_across(c, above).start()
+
+    def relay_all(c):
+        for distance in range(1, depth):
+            at = c + depth - distance
+
+            @pl.when((at >= 0) & (at < chunks))
+            def _():
+                if distance == 1:
+                    q_arrival(at, 1, row).wait_recv()
+                    q_swap(at).start()
+                relay(at, distance)
 
     start_q(0)
     pool_remote().start()
@@ -251,12 +301,7 @@
 
     loop(chunks - 1, start_later)
 
-    def forward(c):
-        for step in range(1, depth):
-            q_copy(c, step).wait_recv()
-            q_forward(c, step).start()
-
-    forward(0)
+    loop(depth - 1, lambda c: relay_all(c + 1 - depth))
     q_local().wait()
     pool_local().wait()
     pool_remote().wait()
@@ -303,13 +348,12 @@
         return mixed / total, highest, total
 
     def do_chunk(c):
-        @pl.when(c + 1 < chunks)
-        def _():
-            forward(c + 1)
-
-        q_copy(c, 0).wait_recv()
-        for step in range(1, depth):
-            q_forward(c, step).wait_recv()
+        for source in range(depth):
+
+            @pl.when(row != source)
+            def _():
+                q_arrival(c, 1, source).wait_recv()
+
         suffix_local(c).wait()
         suffix_remote(c).wait()
         kept = jnp.zeros((heads, 128), jnp.float32)
@@ -371,6 +415,8 @@
             zstat_copy(c, step).start()
 
     def stage(c):
+        relay_all(c)
+
         @pl.when(c < chunks)
         def _():
             do_chunk(c)
@@ -412,10 +458,21 @@
     loop(chunks, finish)
 
     def drain(c):
-        for step in range(depth):
-            q_copy(c, step).wait_send()
-        for step in range(1, depth):
-            q_forward(c, step).wait_send()
+        for source in range(depth):
+
+            @pl.when((source <= row) & (row + 1 < depth))
+            def _():
+                q_up(c, source).wait_send()
+
+            @pl.when((source >= row) & (row > 0))
+            def _():
+                q_down(c, source).wait_send()
+
+            @pl.when(source != twin)
+            def _():
+                q_across(c, source).wait_send()
+
+        q_swap(c).wait_send()
         y_copy(c).wait_send()
         ystat_copy(c).wait_send()
         for step in range(1, depth):
@@ -470,7 +527,7 @@
             dma((2 + chunks,)),
             dma((2,)),
             dma((2, chunks)),
-            dma((chips, chunks)),
+            dma((3 * depth + 1, chunks)),
             dma((chips, chunks)),
             dma((4, chunks)),
             dma((4, depth - 1, chunks)),

time: 77.7 us -> 78.2 us (level)
  no operation moved by 1% of the time
where the time goes in v3:
time: 78.2 us; the launch traced here: 78 us
  Pallas kernels  74.3 us (95%)
  local copies, waits for them, and re-layouts  2.37 us (3%)
  other arithmetic  1.29 us (2%)
    pallas_call x1, Pallas kernels, fused_body(): pl.pallas_call(functools.partial(kernel, chips), out_shape=jax.ShapeDtype...  74.3 us
    unnamed x1, local copies, waits for them, and re-layouts  1.67 us

profile of v3, /device:TPU:0, one launch (start us, length us, event | category | flops | bytes accessed | tf_op | source)
XLA Modules:
  0.0 78.0 jit_solution(4251175274370120345)
XLA Ops:
  0.0 0.7 add_select_fusion
  0.7 0.1 fusion.4
  0.8 0.1 fusion
  0.9 0.2 multiply_reduce_fusion
  1.1 0.2 select_reduce_fusion
  1.3 0.7 copy.10
  2.0 74.3 %shard_map.64 = bf16[16,16,512]{2,1,0:T(8,128)(2,1)} custom-call(s32[16,4]{1,0:T(8,128)} %bitcast.7, s32[32]{0:T(128)} %prefix_ref.1, s32[32]{0:T(128)} %length_ref.1, bf16[16,16,576]{2,1,0:T(8,128)(2,1)} %bitcast.6, bf16[32,64,576]{2,1,0:T(8,128)(2,1)} %pool_hbm.1, bf16[32,576,128]{2,1,0:T(8,128)(2,1)} %bitcast.4), custom_call_target="tpu_custom_call" | custom-call | tf_op jit(solution)/shard_map/pallas_call | solution.py:508
  76.3 1.7 %copy.13 = bf16[32,8,512]{2,1,0:T(8,128)(2,1)} copy(bf16[32,8,512]{2,1,0:T(8,128)(2,1)} %bitcast.5) | data formatting | bytes 524288
  (2 shorter events, 0.0 us)
